TPU v7x, 8 devices: a whole 2x2x1 slice. The times are simulated.
8 devices in a mesh: tp: 2 (over z, y), side: 2 (over x), rep: 2 (over core).
Axes of the slice: x: 2, y: 2, z: 1, core: 2. Of those that a mesh axis runs over, the one named last changes fastest.
Arguments:
- w_up: float32 [2, 1, 2048, 11008], P('side', None, ('rep', 'tp'))
- w_down: float32 [2, 1, 11008, 2048], P('side', None, None, ('rep', 'tp'))
- g_up: float32 [2, 1, 2048, 11008], P('side', None, ('rep', 'tp'))
- g_down: float32 [2, 1, 11008, 2048], P('side', None, None, ('rep', 'tp'))
- learn_rate: float32 [2], P('side')
- prompts: bfloat16 [2, 2, 8192, 2048], P('side', 'rep')
Outputs:
- output 1: float32 [2, 1, 2048, 11008], P('side', None, ('rep', 'tp'))
- output 2: float32 [2, 1, 11008, 2048], P('side', None, None, ('rep', 'tp'))
- output 3: bfloat16 [2, 2, 8192, 2048], P('side', 'rep')
All inputs are finite; a program needn't handle non-finite values.
Results may differ from a plain program's by a relative error of at most 0.001.
Values are sent between devices in bfloat16 or wider.
A program may use at most 1 GiB of HBM per device.

v0:
```python
import jax
import jax.numpy as jnp
from jax import lax
from jax.sharding import PartitionSpec as P


def solution(mesh):
    up_spec = P("side", None, ("rep", "tp"), None)
    down_spec = P("side", None, None, ("rep", "tp"))
    tok_spec = P("side", "rep", None, None)

    def device_step(w_up, w_down, g_up, g_down, learn_rate, prompts):
        is_trainer = lax.axis_index("side") == 0
        rate = learn_rate[0]
        new_up = jnp.where(is_trainer, w_up - rate * g_up, 0.0)
        new_down = jnp.where(is_trainer, w_down - rate * g_down, 0.0)
        recv_up = lax.ppermute(new_up[0].astype(jnp.bfloat16), "side", perm=[(0, 1)])
        recv_down = lax.ppermute(new_down[0].astype(jnp.bfloat16), "side", perm=[(0, 1)])
        band_up = lax.all_to_all(recv_up, "tp", 2, 1, tiled=True)
        band_down = lax.all_to_all(recv_down, "tp", 1, 2, tiled=True)
        full_up = lax.all_gather(band_up, "rep", axis=1, tiled=True)
        full_down = lax.all_gather(band_down, "rep", axis=2, tiled=True)
        hidden = prompts[0, 0]
        for layer in range(full_up.shape[0]):
            pre_act = jnp.dot(hidden, full_up[layer], preferred_element_type=jnp.float32)
            act_up = jax.nn.gelu(pre_act, approximate=True).astype(jnp.bfloat16)
            part_sum = jnp.dot(act_up, full_down[layer], preferred_element_type=jnp.float32)
            part_sum = lax.psum(part_sum, "tp")
            hidden = (hidden.astype(jnp.float32) + part_sum).astype(jnp.bfloat16)
        gen_out = jnp.where(is_trainer, jnp.zeros_like(hidden), hidden)
        return new_up, new_down, gen_out[None, None]

    return jax.shard_map(
        device_step,
        mesh=mesh,
        in_specs=(up_spec, down_spec, up_spec, down_spec, P("side"), tok_spec),
        out_specs=(up_spec, down_spec, tok_spec),
        check_vma=False,
    )
```

profile of v0, /device:TPU:0, one launch (start us, length us, event | category | flops | bytes accessed | tf_op | source)
XLA Modules:
  0.0 3203.8 jit_solution(8100139295891882191)
XLA Ops:
  7.2 0.0 all-gather.3.cloned.1.call-start
  7.9 23.2 convert_bitcast_fusion.1
  31.0 9.5 collective-permute-start
  40.5 237.2 %collective-permute-done = bf16[1,512,11008]{2,1,0:T(8,128)(2,1)} collective-permute-done((bf16[1,512,11008]{2,1,0:T(8,128)(2,1)S(1)}, bf16[1,512,11008]{2,1,0:T(8,128)(2,1)}, u32[]{:S(2)}, u32[]{:S(2)}) %collective-permute-start) | collective-permute-done | bytes 11272224 | tf_op jit(solution)/shard_map/ppermute | solution.py:17
  277.7 46.5 %copy.19 = bf16[1,512,11008]{1,0,2:T(2,128)(2,1)} copy(bf16[1,512,11008]{2,1,0:T(8,128)(2,1)} %collective-permute-done) | data formatting | bytes 22544384 | tf_op jit(solution)/shard_map/ppermute | solution.py:17
  324.3 0.5 broadcast
  324.8 72.8 %reduce = bf16[11008,512]{1,0:T(8,128)(2,1)} reduce(bf16[11008,1,512]{2,1,0:T(2,128)(2,1)} %bitcast.36, bf16[]{:T(256)} %broadcast), dimensions={1}, to_apply=%bitcast.27.reduce_sub_computation | reduce | bytes 22544386
  397.6 18.2 reshape.32
  415.8 136.2 %all_to_all.36 = bf16[2,2,1409024]{2,1,0:T(2,128)(2,1)} all-to-all(bf16[2,2,1409024]{2,1,0:T(2,128)(2,1)} %reshape.32), channel_id=1, replica_groups=mesh['tp'=2,'side'=2,'rep'=2] {'tp'}, dimensions={0} | all-to-all | bytes 22544384 | tf_op jit(solution)/shard_map/all_to_all | solution.py:19
  552.0 23.3 reshape.33
  575.3 14.3 copy.23
  589.5 14.6 copy.20
  604.2 0.0 all-gather.5.cloned.1.call-start
  604.2 23.0 convert_bitcast_fusion
  627.3 17.6 collective-permute-start.1
  644.9 226.9 %collective-permute-done.1 = bf16[1,11008,512]{2,1,0:T(8,128)(2,1)S(1)} collective-permute-done((bf16[1,11008,512]{2,1,0:T(8,128)(2,1)S(1)}, bf16[1,11008,512]{2,1,0:T(8,128)(2,1)S(1)}, u32[]{:S(2)}, u32[]{:S(2)}) %collective-permute-start.1) | collective-permute-done | bytes 11272224 | tf_op jit(solution)/shard_map/ppermute | solution.py:18
  871.7 96.2 %copy.26 = bf16[1,11008,512]{2,0,1:T(2,128)(2,1)} copy(bf16[1,11008,512]{2,1,0:T(8,128)(2,1)S(1)} %collective-permute-done.1) | data formatting | bytes 22544384 | tf_op jit(solution)/shard_map/ppermute | solution.py:18
  967.9 72.7 %reduce.1 = bf16[11008,512]{1,0:T(8,128)(2,1)} reduce(bf16[11008,1,512]{2,1,0:T(2,128)(2,1)} %bitcast.37, bf16[]{:T(256)} %broadcast), dimensions={1}, to_apply=%bitcast.33.reduce_sub_computation | reduce | bytes 22544386
  1040.6 18.2 reshape.34
  1058.8 134.3 %all_to_all.37 = bf16[2,2,1409024]{2,1,0:T(2,128)(2,1)} all-to-all(bf16[2,2,1409024]{2,1,0:T(2,128)(2,1)} %reshape.34), channel_id=1, replica_groups=mesh['tp'=2,'side'=2,'rep'=2] {'tp'}, dimensions={0} | all-to-all | bytes 22544384 | tf_op jit(solution)/shard_map/all_to_all | solution.py:20
  1193.2 23.3 reshape.35
  1216.5 14.4 copy.24
  1230.8 15.6 copy.22
  1246.4 0.0 all-gather.5.cloned.1.call-update
  1246.4 0.0 all-reduce.2.cloned.1.call-start
  1246.5 0.0 all-gather.3.cloned.1.call-done
  1246.5 249.8 %fusion.7 = bf16[8192,5504]{0,1:T(8,128)(2,1)} fusion(bf16[1,1,8192,2048]{3,2,1,0:T(8,128)(2,1)} %param.11, bf16[1,2048,5504]{2,1,0:T(8,128)(2,1)} %all-gather.3.cloned.1.call-done), kind=kOutput, calls=%fused_computation.8 | convolution fusion | flops 185089392640 | bytes 146276352 | tf_op jit(solution)/shard_map/dot_general | solution.py:25
  1496.3 0.0 all-gather.5.cloned.1.call-done
  1496.3 205.5 %fusion.11 = f32[8192,2048]{1,0:T(8,128)} fusion(bf16[8192,5504]{0,1:T(8,128)(2,1)} %fusion.7, bf16[1,5504,2048]{1,2,0:T(8,128)(2,1)} %all-gather.5.cloned.1.call-done), kind=kOutput, calls=%fused_computation.13 | convolution fusion | flops 184683593728 | bytes 179830784 | tf_op jit(solution)/shard_map/dot_general | solution.py:27
  1701.8 0.0 all-reduce.2.cloned.1.call-update
  1701.8 1452.6 %all-reduce.2.cloned.1.call-done = f32[8192,2048]{1,0:T(8,128)} async-done(((f32[8192,2048]{1,0:T(8,128)}), f32[8192,2048]{1,0:T(8,128)}) %all-reduce.2.cloned.1.call-update) | async-done | bytes 67108880 | tf_op jit(solution)/shard_map/psum | solution.py:28
  3154.5 42.6 %fusion.9 = bf16[1,1,8192,2048]{3,2,1,0:T(8,128)(2,1)} fusion(f32[8192,2048]{1,0:T(8,128)} %all-reduce.2.cloned.1.call-done, bf16[1,1,8192,2048]{3,2,1,0:T(8,128)(2,1)} %param.11, pred[]{:T(512)S(6)} %eq.3), kind=kLoop, calls=%fused_computation.11 | loop fusion | flops 67108864 | bytes 134217728 | tf_op jit(solution)/shard_map/broadcast_in_dim | solution.py:31
  (1 shorter events, 0.0 us)
Async XLA Ops:
  7.2 1239.3 %all-gather.3.cloned.1.call-start = ((), (), s32[]{:S(2)}) async-start(), calls=%async_computation.2 | async-start | bytes 33816576 | tf_op jit(solution)/shard_map/all_gather | solution.py:21
  31.0 246.7 %collective-permute-start = (bf16[1,512,11008]{2,1,0:T(8,128)(2,1)S(1)}, bf16[1,512,11008]{2,1,0:T(8,128)(2,1)}, u32[]{:S(2)}, u32[]{:S(2)}) collective-permute-start(bf16[1,512,11008]{2,1,0:T(8,128)(2,1)S(1)} %get-tuple-element.11), channel_id=1, source_target_pairs={{0,2},{1,3},{4,6},{5,7}} | collective-permute-start | bytes 33816584 | tf_op jit(solution)/shard_map/ppermute | solution.py:17
  604.2 892.1 %all-gather.5.cloned.1.call-start = ((), (), s32[]{:S(2)}) async-start(), calls=%async_computation.3 | async-start | bytes 33816576 | tf_op jit(solution)/shard_map/all_gather | solution.py:22
  627.3 244.5 %collective-permute-start.1 = (bf16[1,11008,512]{2,1,0:T(8,128)(2,1)S(1)}, bf16[1,11008,512]{2,1,0:T(8,128)(2,1)S(1)}, u32[]{:S(2)}, u32[]{:S(2)}) collective-permute-start(bf16[1,11008,512]{2,1,0:T(8,128)(2,1)S(1)} %get-tuple-element.9), channel_id=1, source_target_pairs={{0,2},{1,3},{4,6},{5,7}} | collective-permute-start | bytes 33816584 | tf_op jit(solution)/shard_map/ppermute | solution.py:18
  1246.4 1908.0 %all-reduce.2.cloned.1.call-start = ((), (), s32[]{:S(2)}) async-start(), calls=%async_computation.4 | async-start | bytes 134217728 | tf_op jit(solution)/shard_map/psum | solution.py:28
Sparse Core Ops, SparseCore 0:
  604.3 36.0 all-gather.2
  1246.5 35.9 all-gather.4
  1702.0 1452.4 all-reduce.1
where the time goes:
time: 3210 us; the launch traced here: 3200 us
  waiting for transfers between devices  1920 us (60%)
  matrix products  455 us (14%)
  local copies, waits for them, and re-layouts  285 us (9%)
  blocking collectives  271 us (8%)
  other arithmetic  234 us (7%)
    psum x1, waiting for transfers between devices, device_step(): part_sum = lax.psum(part_sum, 'tp')  1450 us
    dot_general x1, matrix products, device_step(): jnp.dot(hidden, full_up[layer], preferred_element_type=jnp.float32)  250 us
    ppermute x1, waiting for transfers between devices, device_step(): lax.ppermute(new_up[0].astype(jnp.bfloat16), 'side', perm=[(0, 1)])  237 us
    ppermute x1, waiting for transfers between devices, device_step(): lax.ppermute(new_down[0].astype(jnp.bfloat16), 'side', perm=[(0, 1)])  227 us
    dot_general x1, matrix products, device_step(): jnp.dot(act_up, full_down[layer], preferred_element_type=jnp.float32)  206 us
    unnamed x2, other arithmetic  145 us
    all_to_all x1, blocking collectives, device_step(): band_up = lax.all_to_all(recv_up, 'tp', 2, 1, tiled=True)  136 us
    all_to_all x1, blocking collectives, device_step(): band_down = lax.all_to_all(recv_down, 'tp', 1, 2, tiled=True)  134 us
  transfers between devices with their start and end apart: 5, of which 3 were waited for; matrix products, arithmetic and copies ran while one was open for 16% of the time, Pallas kernels for 0%

commit v1 on v0

v1 whole, which is shorter than its diff:
```python
import jax
import jax.numpy as jnp
from jax import lax
from jax.sharding import PartitionSpec as P

NUM_CHUNKS = 4
TILE = 256


def solution(mesh):
    up_spec = P("side", None, ("rep", "tp"), None)
    down_spec = P("side", None, None, ("rep", "tp"))
    tok_spec = P("side", "rep", None, None)

    def device_step(w_up, w_down, g_up, g_down, learn_rate, prompts):
        rate = learn_rate[0]
        new_up = w_up - rate * g_up
        new_down = w_down - rate * g_down
        cast_up = new_up[0].astype(jnp.bfloat16)
        cast_down = new_down[0].astype(jnp.bfloat16)
        layers, _, hidden_dim = cast_up.shape
        tiles = hidden_dim // TILE
        edges = [TILE * (tiles * k // NUM_CHUNKS) for k in range(NUM_CHUNKS)] + [hidden_dim]
        tp_size = lax.axis_size("tp")
        rows = prompts.shape[2] // tp_size
        hidden = lax.dynamic_slice_in_dim(prompts[0, 0], lax.axis_index("tp") * rows, rows, 0)
        for layer in range(layers):
            total = hidden.astype(jnp.float32)
            part_sum = None
            for lo, hi in zip(edges[:-1], edges[1:]):
                up = lax.ppermute(cast_up[layer, :, lo:hi], "side", perm=[(0, 1)])
                down = lax.ppermute(cast_down[layer, lo:hi, :], "side", perm=[(0, 1)])
                up_other = lax.ppermute(up, "tp", perm=[(0, 1), (1, 0)])
                down_other = lax.ppermute(down, "tp", perm=[(0, 1), (1, 0)])
                first = lax.axis_index("tp") == 0
                up = jnp.concatenate([jnp.where(first, up, up_other), jnp.where(first, up_other, up)], 0)
                down = jnp.concatenate([jnp.where(first, down, down_other), jnp.where(first, down_other, down)], 1)
                up_other = lax.ppermute(up, "rep", perm=[(0, 1), (1, 0)])
                down_other = lax.ppermute(down, "rep", perm=[(0, 1), (1, 0)])
                first = lax.axis_index("rep") == 0
                up = jnp.concatenate([jnp.where(first, up, up_other), jnp.where(first, up_other, up)], 0)
                down = jnp.concatenate([jnp.where(first, down, down_other), jnp.where(first, down_other, down)], 1)
                pre_act = jnp.dot(hidden, up, preferred_element_type=jnp.float32)
                act_up = jax.nn.gelu(pre_act, approximate=True).astype(jnp.bfloat16)
                part = jnp.dot(act_up, down, preferred_element_type=jnp.float32)
                part_sum = part if part_sum is None else part_sum + part
            hidden = (total + part_sum).astype(jnp.bfloat16)
        other = lax.ppermute(hidden, "tp", perm=[(0, 1), (1, 0)])
        first = lax.axis_index("tp") == 0
        gen_out = jnp.concatenate([jnp.where(first, hidden, other), jnp.where(first, other, hidden)], 0)
        return new_up, new_down, gen_out[None, None]

    return jax.shard_map(
        device_step,
        mesh=mesh,
        in_specs=(up_spec, down_spec, up_spec, down_spec, P("side"), tok_spec),
        out_specs=(up_spec, down_spec, tok_spec),
        check_vma=False,
    )
```

time: 3210 us -> 1760 us (0.55)
  waiting for transfers between devices: 1920 us -> 981 us
  local copies, waits for them, and re-layouts: 285 us -> 8.77 us
  blocking collectives: 271 us -> 0 us
    psum x1 -> x0, waiting for transfers between devices: 1450 us -> none  [device_step(): part_sum = lax.psum(part_sum, 'tp')]
    ppermute x2 -> x25, waiting for transfers between devices: 464 us -> 981 us  [the longest x1 361 us: device_step(): other = lax.ppermute(hidden, 'tp', perm=[(0, 1), (1, 0)])]
    all_to_all x2 -> x0, blocking collectives: 271 us -> none  [the longest x1 136 us: device_step(): band_up = lax.all_to_all(recv_up, 'tp', 2, 1, tiled=True)]
    unnamed x2 -> x0, other arithmetic: 145 us -> none
    ppermute x2 -> x0, local copies, waits for them, and re-layouts: 143 us -> none  [the longest x1 96.2 us: device_step(): lax.ppermute(new_down[0].astype(jnp.bfloat16), 'side', perm=[(0, 1)])]
    select_n x0 -> x15, other arithmetic: none -> 128 us  [the longest x7 58 us: device_step(): jnp.where(first, up, up_other)]
    unnamed x7 -> x48, local copies, waits for them, and re-layouts: 112 us -> 1.44 us
    concatenate x0 -> x8, other arithmetic: none -> 34.7 us  [the longest x4 20.2 us: device_step(): jnp.concatenate([jnp.where(first, down, down_other), jnp.where(first, dow...]
  transfers between devices with their start and end apart: 5 -> 25, of which waited for: 3 -> 14; matrix products, arithmetic and copies ran while one was open for 16% -> 33% of each run, Pallas kernels for 0% -> 0%
where the time goes in v1:
time: 1760 us; the launch traced here: 1750 us
  waiting for transfers between devices  981 us (56%)
  matrix products  478 us (27%)
  other arithmetic  233 us (13%)
  starting transfers between devices  46.4 us (3%)
    ppermute x1, waiting for transfers between devices, device_step(): other = lax.ppermute(hidden, 'tp', perm=[(0, 1), (1, 0)])  361 us
    dot_general x4, matrix products, device_step(): part = jnp.dot(act_up, down, preferred_element_type=jnp.float32)  251 us
    dot_general x4, matrix products, device_step(): pre_act = jnp.dot(hidden, up, preferred_element_type=jnp.float32)  227 us
    ppermute x4, waiting for transfers between devices, device_step(): down = lax.ppermute(cast_down[layer, lo:hi, :], 'side', perm=[(0, 1)])  216 us
    ppermute x4, waiting for transfers between devices, device_step(): up = lax.ppermute(cast_up[layer, :, lo:hi], 'side', perm=[(0, 1)])  190 us
    ppermute x4, waiting for transfers between devices, device_step(): down_other = lax.ppermute(down, 'tp', perm=[(0, 1), (1, 0)])  163 us
    select_n x7, other arithmetic, device_step(): jnp.where(first, up, up_other)  58 us
    select_n x7, other arithmetic, device_step(): jnp.where(first, down, down_other)  52.1 us
  transfers between devices with their start and end apart: 25, of which 14 were waited for; matrix products, arithmetic and copies ran while one was open for 33% of the time, Pallas kernels for 0%

profile of v1, /device:TPU:0, one launch (start us, length us, event | category | flops | bytes accessed | tf_op | source)
XLA Modules:
  0.0 1748.9 jit_solution(2564063353501843917)
XLA Ops:
  1.3 23.1 %convert_bitcast_fusion.1 = (bf16[1,512,11008]{2,1,0:T(8,128)(2,1)S(1)}, f32[1,1,512,11008]{3,2,1,0:T(8,128)}) fusion(f32[1,1,512,11008]{3,2,1,0:T(8,128)} %param.6, f32[1,1,512,11008]{3,2,1,0:T(8,128)} %param.8, f32[]{:T(128)} %bitcast.41), kind=kLoop, calls=%fused_computation.73 | loop fusion | flops 16908288 | bytes 78905344 | tf_op jit(solution)/shard_map/convert_element_type | solution.py:19
  32.8 23.0 %convert_bitcast_fusion = (bf16[1,11008,512]{2,1,0:T(8,128)(2,1)S(1)}, f32[1,1,11008,512]{3,2,1,0:T(8,128)}) fusion(f32[1,1,11008,512]{3,2,1,0:T(8,128)} %param.7, f32[1,1,11008,512]{3,2,1,0:T(8,128)} %param.9, f32[]{:T(128)} %bitcast.42), kind=kLoop, calls=%fused_computation.72 | loop fusion | flops 16908288 | bytes 78905344 | tf_op jit(solution)/shard_map/convert_element_type | solution.py:20
  71.3 17.2 collective-permute-done
  94.5 50.2 %collective-permute-done.3 = bf16[2560,512]{1,0:T(8,128)(2,1)} collective-permute-done((bf16[2560,512]{1,0:T(8,128)(2,1)S(1)}, bf16[2560,512]{1,0:T(8,128)(2,1)}, u32[]{:S(2)}, u32[]{:S(2)}) %collective-permute-start.3) | collective-permute-done | bytes 2621472 | tf_op jit(solution)/shard_map/ppermute | solution.py:32
  146.2 60.3 %collective-permute-done.18 = bf16[512,2816]{1,0:T(8,128)(2,1)} collective-permute-done((bf16[512,2816]{1,0:T(8,128)(2,1)S(1)}, bf16[512,2816]{1,0:T(8,128)(2,1)}, u32[]{:S(2)}, u32[]{:S(2)}) %collective-permute-start.18) | collective-permute-done | bytes 2883616 | tf_op jit(solution)/shard_map/ppermute | solution.py:31
  212.5 55.8 %collective-permute-done.12 = bf16[512,2816]{1,0:T(8,128)(2,1)} collective-permute-done((bf16[512,2816]{1,0:T(8,128)(2,1)S(1)}, bf16[512,2816]{1,0:T(8,128)(2,1)}, u32[]{:S(2)}, u32[]{:S(2)}) %collective-permute-start.12) | collective-permute-done | bytes 2883616 | tf_op jit(solution)/shard_map/ppermute | solution.py:31
  269.8 60.3 %collective-permute-done.21 = bf16[2816,512]{1,0:T(8,128)(2,1)S(1)} collective-permute-done((bf16[2816,512]{1,0:T(8,128)(2,1)}, bf16[2816,512]{1,0:T(8,128)(2,1)S(1)}, u32[]{:S(2)}, u32[]{:S(2)}) %collective-permute-start.21) | collective-permute-done | bytes 2883616 | tf_op jit(solution)/shard_map/ppermute | solution.py:32
  336.0 55.8 %collective-permute-done.15 = bf16[2816,512]{1,0:T(8,128)(2,1)} collective-permute-done((bf16[2816,512]{1,0:T(8,128)(2,1)}, bf16[2816,512]{1,0:T(8,128)(2,1)}, u32[]{:S(2)}, u32[]{:S(2)}) %collective-permute-start.15) | collective-permute-done | bytes 2883616 | tf_op jit(solution)/shard_map/ppermute | solution.py:32
  396.8 56.9 %collective-permute-done.6 = bf16[512,2816]{1,0:T(8,128)(2,1)} collective-permute-done((bf16[512,2816]{1,0:T(8,128)(2,1)}, bf16[512,2816]{1,0:T(8,128)(2,1)}, u32[]{:S(2)}, u32[]{:S(2)}) %collective-permute-start.6) | collective-permute-done | bytes 2883616 | tf_op jit(solution)/shard_map/ppermute | solution.py:31
  464.6 49.7 %collective-permute-done.9 = bf16[2816,512]{1,0:T(8,128)(2,1)} collective-permute-done((bf16[2816,512]{1,0:T(8,128)(2,1)}, bf16[2816,512]{1,0:T(8,128)(2,1)}, u32[]{:S(2)}, u32[]{:S(2)}) %collective-permute-start.9) | collective-permute-done | bytes 2883616 | tf_op jit(solution)/shard_map/ppermute | solution.py:32
  527.9 52.9 %collective-permute-done.22 = bf16[2816,512]{1,0:T(8,128)(2,1)} collective-permute-done((bf16[2816,512]{1,0:T(8,128)(2,1)S(1)}, bf16[2816,512]{1,0:T(8,128)(2,1)}, u32[]{:S(2)}, u32[]{:S(2)}) %collective-permute-start.22) | collective-permute-done | bytes 2883616 | tf_op jit(solution)/shard_map/ppermute | solution.py:34
  580.8 61.8 %collective-permute-done.16 = bf16[2816,512]{1,0:T(8,128)(2,1)} collective-permute-done((bf16[2816,512]{1,0:T(8,128)(2,1)}, bf16[2816,512]{1,0:T(8,128)(2,1)}, u32[]{:S(2)}, u32[]{:S(2)}) %collective-permute-start.16) | collective-permute-done | bytes 2883616 | tf_op jit(solution)/shard_map/ppermute | solution.py:34
  656.2 48.2 %collective-permute-done.7 = bf16[512,2816]{1,0:T(8,128)(2,1)} collective-permute-done((bf16[512,2816]{1,0:T(8,128)(2,1)}, bf16[512,2816]{1,0:T(8,128)(2,1)}, u32[]{:S(2)}, u32[]{:S(2)}) %collective-permute-start.7) | collective-permute-done | bytes 2883616 | tf_op jit(solution)/shard_map/ppermute | solution.py:33
  714.7 48.3 %collective-permute-done.10 = bf16[2816,512]{1,0:T(8,128)(2,1)} collective-permute-done((bf16[2816,512]{1,0:T(8,128)(2,1)}, bf16[2816,512]{1,0:T(8,128)(2,1)}, u32[]{:S(2)}, u32[]{:S(2)}) %collective-permute-start.10) | collective-permute-done | bytes 2883616 | tf_op jit(solution)/shard_map/ppermute | solution.py:34
  781.2 10.1 broadcast_select_fusion.17
  791.4 52.5 %fusion.48 = f32[4096,2560]{1,0:T(8,128)} fusion(bf16[1024,2560]{1,0:T(8,128)(2,1)} %get-tuple-element.30, bf16[1024,2560]{1,0:T(8,128)(2,1)} %get-tuple-element.29, bf16[1,1,8192,2048]{3,2,1,0:T(8,128)(2,1)} %param.11, s32[]{:T(128)S(6)} %select_n.176), kind=kOutput, calls=%fused_computation.50 | convolution fusion | flops 42970644480 | bytes 69206016 | tf_op jit(solution)/shard_map/dot_general | solution.py:43
  853.4 57.1 %fusion.38 = f32[4096,2048]{1,0:T(8,128)} fusion(f32[4096,2560]{1,0:T(8,128)} %fusion.48, bf16[2560,1024]{1,0:T(8,128)(2,1)} %get-tuple-element.28, bf16[2560,1024]{1,0:T(8,128)(2,1)} %get-tuple-element.27), kind=kOutput, calls=%fused_computation.43 | convolution fusion | flops 43065016320 | bytes 85983232 | tf_op jit(solution)/shard_map/dot_general | solution.py:45
  910.5 11.3 broadcast_select_fusion.11
  921.8 58.1 %fusion.44 = f32[4096,2816]{1,0:T(8,128)} fusion(bf16[1024,2816]{1,0:T(8,128)(2,1)} %get-tuple-element.20, bf16[1024,2816]{1,0:T(8,128)(2,1)} %get-tuple-element.19, bf16[1,1,8192,2048]{3,2,1,0:T(8,128)(2,1)} %param.11, s32[]{:T(128)S(6)} %select_n.176), kind=kOutput, calls=%fused_computation.46 | convolution fusion | flops 47267708928 | bytes 74448896 | tf_op jit(solution)/shard_map/dot_general | solution.py:43
  979.9 9.7 broadcast_select_fusion.5
  989.7 62.1 %fusion.34 = f32[4096,2048]{1,0:T(8,128)} fusion(f32[4096,2816]{1,0:T(8,128)} %fusion.44, bf16[2816,1024]{1,0:T(8,128)(2,1)} %get-tuple-element.18, bf16[2816,1024]{1,0:T(8,128)(2,1)} %get-tuple-element.17), kind=kOutput, calls=%fused_computation.39 | convolution fusion | flops 47371517952 | bytes 91226112 | tf_op jit(solution)/shard_map/dot_general | solution.py:45
  1051.8 12.2 broadcast_select_fusion.13
  1064.0 58.1 %fusion.46 = f32[4096,2816]{1,0:T(8,128)} fusion(bf16[1024,2816]{1,0:T(8,128)(2,1)} %get-tuple-element.16, bf16[1024,2816]{1,0:T(8,128)(2,1)} %get-tuple-element.15, bf16[1,1,8192,2048]{3,2,1,0:T(8,128)(2,1)} %param.11, s32[]{:T(128)S(6)} %select_n.176), kind=kOutput, calls=%fused_computation.48 | convolution fusion | flops 47267708928 | bytes 74448896 | tf_op jit(solution)/shard_map/dot_general | solution.py:43
  1122.0 9.7 broadcast_select_fusion.7
  1131.7 61.7 %fusion.36 = f32[4096,2048]{1,0:T(8,128)} fusion(f32[4096,2816]{1,0:T(8,128)} %fusion.46, bf16[2816,1024]{1,0:T(8,128)(2,1)} %get-tuple-element.14, bf16[2816,1024]{1,0:T(8,128)(2,1)} %get-tuple-element.13), kind=kOutput, calls=%fused_computation.40 | convolution fusion | flops 47371517952 | bytes 91226112 | tf_op jit(solution)/shard_map/dot_general | solution.py:45
  1193.5 12.2 broadcast_select_fusion.9
  1205.6 58.1 %fusion.42 = f32[4096,2816]{1,0:T(8,128)} fusion(bf16[1024,2816]{1,0:T(8,128)(2,1)} %get-tuple-element.12, bf16[1024,2816]{1,0:T(8,128)(2,1)} %get-tuple-element.11, bf16[1,1,8192,2048]{3,2,1,0:T(8,128)(2,1)} %param.11, s32[]{:T(128)S(6)} %select_n.176), kind=kOutput, calls=%fused_computation.44 | convolution fusion | flops 47267708928 | bytes 74448896 | tf_op jit(solution)/shard_map/dot_general | solution.py:43
  1263.8 9.8 broadcast_select_fusion.3
  1273.5 70.4 %add_convert_fusion = bf16[4096,2048]{1,0:T(8,128)(2,1)} fusion(f32[4096,2048]{1,0:T(8,128)} %fusion.34, f32[4096,2048]{1,0:T(8,128)} %fusion.38, f32[4096,2048]{1,0:T(8,128)} %fusion.36, f32[4096,2816]{1,0:T(8,128)} %fusion.42, bf16[2816,1024]{1,0:T(8,128)(2,1)} %get-tuple-element.10, bf16[2816,1024]{1,0:T(8,128)(2,1)} %get-tuple-element.9, ...), kind=kOutput, calls=%fused_computation.37 | convolution fusion | flops 47421849600 | bytes 191889408 | tf_op jit(solution)/shard_map/dot_general | solution.py:45
  1345.5 361.1 %collective-permute-done.24 = bf16[4096,2048]{1,0:T(8,128)(2,1)S(1)} collective-permute-done((bf16[4096,2048]{1,0:T(8,128)(2,1)}, bf16[4096,2048]{1,0:T(8,128)(2,1)S(1)}, u32[]{:S(2)}, u32[]{:S(2)}) %collective-permute-start.24) | collective-permute-done | bytes 16777248 | tf_op jit(solution)/shard_map/ppermute | solution.py:48
  1706.5 18.2 %broadcast_select_fusion.1 = (bf16[4096,2048]{1,0:T(8,128)(2,1)}, bf16[4096,2048]{1,0:T(8,128)(2,1)}) fusion(bf16[4096,2048]{1,0:T(8,128)(2,1)} %add_convert_fusion, bf16[4096,2048]{1,0:T(8,128)(2,1)S(1)} %collective-permute-done.24, pred[]{:T(512)S(6)} %eq.4), kind=kLoop, calls=%fused_computation.53 | loop fusion | flops 16777216 | bytes 67108864 | tf_op jit(solution)/shard_map/jit(_where)/select_n | solution.py:50
  1724.7 23.8 %maximum_bitcast_fusion = bf16[1,1,8192,2048]{3,2,1,0:T(8,128)(2,1)} fusion(bf16[4096,2048]{1,0:T(8,128)(2,1)} %get-tuple-element.8, bf16[4096,2048]{1,0:T(8,128)(2,1)} %get-tuple-element.7), kind=kLoop, calls=%fused_computation.36 | loop fusion | flops 67108864 | bytes 67108864 | tf_op jit(solution)/shard_map/broadcast_in_dim | solution.py:51
  (104 shorter events, 127.7 us)
Async XLA Ops:
  26.0 62.5 %collective-permute-start = (bf16[512,2560]{1,0:T(8,128)(2,1)}, bf16[512,2560]{1,0:T(8,128)(2,1)}, u32[]{:S(2)}, u32[]{:S(2)}) collective-permute-start(bf16[512,2560]{1,0:T(8,128)(2,1)} %slice_bitcast_fusion.7), channel_id=1, source_target_pairs={{0,2},{1,3},{4,6},{5,7}} | collective-permute-start | bytes 7864328 | tf_op jit(solution)/shard_map/ppermute | solution.py:31
  56.0 88.7 %collective-permute-start.3 = (bf16[2560,512]{1,0:T(8,128)(2,1)S(1)}, bf16[2560,512]{1,0:T(8,128)(2,1)}, u32[]{:S(2)}, u32[]{:S(2)}) collective-permute-start(bf16[2560,512]{1,0:T(8,128)(2,1)S(1)} %slice_bitcast_fusion.6), channel_id=1, source_target_pairs={{0,2},{1,3},{4,6},{5,7}} | collective-permute-start | bytes 7864328 | tf_op jit(solution)/shard_map/ppermute | solution.py:32
  60.6 145.8 %collective-permute-start.18 = (bf16[512,2816]{1,0:T(8,128)(2,1)S(1)}, bf16[512,2816]{1,0:T(8,128)(2,1)}, u32[]{:S(2)}, u32[]{:S(2)}) collective-permute-start(bf16[512,2816]{1,0:T(8,128)(2,1)S(1)} %get-tuple-element.24), channel_id=1, source_target_pairs={{0,2},{1,3},{4,6},{5,7}} | collective-permute-start | bytes 8650760 | tf_op jit(solution)/shard_map/ppermute | solution.py:31
  63.5 204.8 %collective-permute-start.12 = (bf16[512,2816]{1,0:T(8,128)(2,1)S(1)}, bf16[512,2816]{1,0:T(8,128)(2,1)}, u32[]{:S(2)}, u32[]{:S(2)}) collective-permute-start(bf16[512,2816]{1,0:T(8,128)(2,1)S(1)} %get-tuple-element.25), channel_id=1, source_target_pairs={{0,2},{1,3},{4,6},{5,7}} | collective-permute-start | bytes 8650760 | tf_op jit(solution)/shard_map/ppermute | solution.py:31
  69.9 260.2 %collective-permute-start.21 = (bf16[2816,512]{1,0:T(8,128)(2,1)}, bf16[2816,512]{1,0:T(8,128)(2,1)S(1)}, u32[]{:S(2)}, u32[]{:S(2)}) collective-permute-start(bf16[2816,512]{1,0:T(8,128)(2,1)} %get-tuple-element.21), channel_id=1, source_target_pairs={{0,2},{1,3},{4,6},{5,7}} | collective-permute-start | bytes 8650760 | tf_op jit(solution)/shard_map/ppermute | solution.py:32
  88.5 303.4 %collective-permute-start.15 = (bf16[2816,512]{1,0:T(8,128)(2,1)}, bf16[2816,512]{1,0:T(8,128)(2,1)}, u32[]{:S(2)}, u32[]{:S(2)}) collective-permute-start(bf16[2816,512]{1,0:T(8,128)(2,1)} %get-tuple-element.22), channel_id=1, source_target_pairs={{0,2},{1,3},{4,6},{5,7}} | collective-permute-start | bytes 8650760 | tf_op jit(solution)/shard_map/ppermute | solution.py:32
  144.7 248.7 %collective-permute-start.1 = (bf16[512,2560]{1,0:T(8,128)(2,1)}, bf16[512,2560]{1,0:T(8,128)(2,1)}, u32[]{:S(2)}, u32[]{:S(2)}) collective-permute-start(bf16[512,2560]{1,0:T(8,128)(2,1)} %collective-permute-done), channel_id=1, source_target_pairs={{0,4},{4,0},{1,5},{5,1},{2,6},{6,2},{3,7},{7,3}} | collective-permute-start | bytes 7864328 | tf_op jit(solution)/shard_map/ppermute | solution.py:33
  206.5 247.2 %collective-permute-start.6 = (bf16[512,2816]{1,0:T(8,128)(2,1)}, bf16[512,2816]{1,0:T(8,128)(2,1)}, u32[]{:S(2)}, u32[]{:S(2)}) collective-permute-start(bf16[512,2816]{1,0:T(8,128)(2,1)} %get-tuple-element.26), channel_id=1, source_target_pairs={{0,2},{1,3},{4,6},{5,7}} | collective-permute-start | bytes 8650760 | tf_op jit(solution)/shard_map/ppermute | solution.py:31
  268.3 186.9 %collective-permute-start.4 = (bf16[2560,512]{1,0:T(8,128)(2,1)}, bf16[2560,512]{1,0:T(8,128)(2,1)}, u32[]{:S(2)}, u32[]{:S(2)}) collective-permute-start(bf16[2560,512]{1,0:T(8,128)(2,1)} %collective-permute-done.3), channel_id=1, source_target_pairs={{0,4},{4,0},{1,5},{5,1},{2,6},{6,2},{3,7},{7,3}} | collective-permute-start | bytes 7864328 | tf_op jit(solution)/shard_map/ppermute | solution.py:34
  330.1 128.5 %copy-start.22 = (bf16[2816,512]{1,0:T(8,128)(2,1)}, bf16[2816,512]{1,0:T(8,128)(2,1)S(1)}, u32[]{:S(2)}) copy-start(bf16[2816,512]{1,0:T(8,128)(2,1)S(1)} %collective-permute-done.21) | copy-start | bytes 8650756
  330.1 184.2 %collective-permute-start.9 = (bf16[2816,512]{1,0:T(8,128)(2,1)}, bf16[2816,512]{1,0:T(8,128)(2,1)}, u32[]{:S(2)}, u32[]{:S(2)}) collective-permute-start(bf16[2816,512]{1,0:T(8,128)(2,1)} %get-tuple-element.23), channel_id=1, source_target_pairs={{0,2},{1,3},{4,6},{5,7}} | collective-permute-start | bytes 8650760 | tf_op jit(solution)/shard_map/ppermute | solution.py:32
  391.9 124.0 %collective-permute-start.19 = (bf16[512,2816]{1,0:T(8,128)(2,1)}, bf16[512,2816]{1,0:T(8,128)(2,1)S(1)}, u32[]{:S(2)}, u32[]{:S(2)}) collective-permute-start(bf16[512,2816]{1,0:T(8,128)(2,1)} %collective-permute-done.18), channel_id=1, source_target_pairs={{0,4},{4,0},{1,5},{5,1},{2,6},{6,2},{3,7},{7,3}} | collective-permute-start | bytes 8650760 | tf_op jit(solution)/shard_map/ppermute | solution.py:33
  393.4 125.6 %collective-permute-start.13 = (bf16[512,2816]{1,0:T(8,128)(2,1)}, bf16[512,2816]{1,0:T(8,128)(2,1)}, u32[]{:S(2)}, u32[]{:S(2)}) collective-permute-start(bf16[512,2816]{1,0:T(8,128)(2,1)} %collective-permute-done.12), channel_id=1, source_target_pairs={{0,4},{4,0},{1,5},{5,1},{2,6},{6,2},{3,7},{7,3}} | collective-permute-start | bytes 8650760 | tf_op jit(solution)/shard_map/ppermute | solution.py:33
  396.8 64.7 %copy-start.15 = (bf16[512,2560]{1,0:T(8,128)(2,1)}, bf16[512,2560]{1,0:T(8,128)(2,1)S(1)}, u32[]{:S(2)}) copy-start(bf16[512,2560]{1,0:T(8,128)(2,1)S(1)} %get-tuple-element.45) | copy-start | bytes 7864324
  396.8 64.7 %copy-start.17 = (bf16[512,2560]{1,0:T(8,128)(2,1)}, bf16[512,2560]{1,0:T(8,128)(2,1)S(1)}, u32[]{:S(2)}) copy-start(bf16[512,2560]{1,0:T(8,128)(2,1)S(1)} %get-tuple-element.46) | copy-start | bytes 7864324
  453.7 127.2 %collective-permute-start.22 = (bf16[2816,512]{1,0:T(8,128)(2,1)S(1)}, bf16[2816,512]{1,0:T(8,128)(2,1)}, u32[]{:S(2)}, u32[]{:S(2)}) collective-permute-start(bf16[2816,512]{1,0:T(8,128)(2,1)S(1)} %collective-permute-done.21), channel_id=1, source_target_pairs={{0,4},{4,0},{1,5},{5,1},{2,6},{6,2},{3,7},{7,3}} | collective-permute-start | bytes 8650760 | tf_op jit(solution)/shard_map/ppermute | solution.py:34
  455.2 187.4 %collective-permute-start.16 = (bf16[2816,512]{1,0:T(8,128)(2,1)}, bf16[2816,512]{1,0:T(8,128)(2,1)}, u32[]{:S(2)}, u32[]{:S(2)}) collective-permute-start(bf16[2816,512]{1,0:T(8,128)(2,1)} %collective-permute-done.15), channel_id=1, source_target_pairs={{0,4},{4,0},{1,5},{5,1},{2,6},{6,2},{3,7},{7,3}} | collective-permute-start | bytes 8650760 | tf_op jit(solution)/shard_map/ppermute | solution.py:34
  514.3 190.1 %collective-permute-start.7 = (bf16[512,2816]{1,0:T(8,128)(2,1)}, bf16[512,2816]{1,0:T(8,128)(2,1)}, u32[]{:S(2)}, u32[]{:S(2)}) collective-permute-start(bf16[512,2816]{1,0:T(8,128)(2,1)} %collective-permute-done.6), channel_id=1, source_target_pairs={{0,4},{4,0},{1,5},{5,1},{2,6},{6,2},{3,7},{7,3}} | collective-permute-start | bytes 8650760 | tf_op jit(solution)/shard_map/ppermute | solution.py:33
  515.8 247.2 %collective-permute-start.10 = (bf16[2816,512]{1,0:T(8,128)(2,1)}, bf16[2816,512]{1,0:T(8,128)(2,1)}, u32[]{:S(2)}, u32[]{:S(2)}) collective-permute-start(bf16[2816,512]{1,0:T(8,128)(2,1)} %collective-permute-done.9), channel_id=1, source_target_pairs={{0,4},{4,0},{1,5},{5,1},{2,6},{6,2},{3,7},{7,3}} | collective-permute-start | bytes 8650760 | tf_op jit(solution)/shard_map/ppermute | solution.py:34
  519.0 261.3 %collective-permute-start.2 = (bf16[1024,2560]{1,0:T(8,128)(2,1)}, bf16[1024,2560]{1,0:T(8,128)(2,1)}, u32[]{:S(2)}, u32[]{:S(2)}) collective-permute-start(bf16[1024,2560]{1,0:T(8,128)(2,1)} %pad_maximum_fusion.6), channel_id=1, source_target_pairs={{0,1},{1,0},{2,3},{3,2},{4,5},{5,4},{6,7},{7,6}} | collective-permute-start | bytes 15728648 | tf_op jit(solution)/shard_map/ppermute | solution.py:38
  523.8 250.1 %copy-start = (bf16[512,2816]{1,0:T(8,128)(2,1)}, bf16[512,2816]{1,0:T(8,128)(2,1)S(1)}, u32[]{:S(2)}) copy-start(bf16[512,2816]{1,0:T(8,128)(2,1)S(1)} %get-tuple-element.33) | copy-start | bytes 8650756
  523.8 250.0 %copy-start.2 = (bf16[512,2816]{1,0:T(8,128)(2,1)}, bf16[512,2816]{1,0:T(8,128)(2,1)S(1)}, u32[]{:S(2)}) copy-start(bf16[512,2816]{1,0:T(8,128)(2,1)S(1)} %get-tuple-element.34) | copy-start | bytes 8650756
  580.8 263.1 %collective-permute-start.5 = (bf16[2560,1024]{1,0:T(8,128)(2,1)}, bf16[2560,1024]{1,0:T(8,128)(2,1)}, u32[]{:S(2)}, u32[]{:S(2)}) collective-permute-start(bf16[2560,1024]{1,0:T(8,128)(2,1)} %pad_maximum_fusion.7), channel_id=1, source_target_pairs={{0,1},{1,0},{2,3},{3,2},{4,5},{5,4},{6,7},{7,6}} | collective-permute-start | bytes 15728648 | tf_op jit(solution)/shard_map/ppermute | solution.py:39
  642.6 267.9 %collective-permute-start.14 = (bf16[1024,2816]{1,0:T(8,128)(2,1)}, bf16[1024,2816]{1,0:T(8,128)(2,1)}, u32[]{:S(2)}, u32[]{:S(2)}) collective-permute-start(bf16[1024,2816]{1,0:T(8,128)(2,1)} %pad_maximum_fusion.2), channel_id=1, source_target_pairs={{0,1},{1,0},{2,3},{3,2},{4,5},{5,4},{6,7},{7,6}} | collective-permute-start | bytes 17301512 | tf_op jit(solution)/shard_map/ppermute | solution.py:38
  648.9 127.7 %copy-start.3 = (bf16[2816,512]{1,0:T(8,128)(2,1)}, bf16[2816,512]{1,0:T(8,128)(2,1)S(1)}, u32[]{:S(2)}) copy-start(bf16[2816,512]{1,0:T(8,128)(2,1)S(1)} %get-tuple-element.31) | copy-start | bytes 8650756
  648.9 127.7 %copy-start.5 = (bf16[2816,512]{1,0:T(8,128)(2,1)}, bf16[2816,512]{1,0:T(8,128)(2,1)S(1)}, u32[]{:S(2)}) copy-start(bf16[2816,512]{1,0:T(8,128)(2,1)S(1)} %get-tuple-element.32) | copy-start | bytes 8650756
  704.4 275.5 %collective-permute-start.17 = (bf16[2816,1024]{1,0:T(8,128)(2,1)}, bf16[2816,1024]{1,0:T(8,128)(2,1)}, u32[]{:S(2)}, u32[]{:S(2)}) collective-permute-start(bf16[2816,1024]{1,0:T(8,128)(2,1)} %pad_maximum_fusion.3), channel_id=1, source_target_pairs={{0,1},{1,0},{2,3},{3,2},{4,5},{5,4},{6,7},{7,6}} | collective-permute-start | bytes 17301512 | tf_op jit(solution)/shard_map/ppermute | solution.py:39
  763.1 288.7 %collective-permute-start.8 = (bf16[1024,2816]{1,0:T(8,128)(2,1)}, bf16[1024,2816]{1,0:T(8,128)(2,1)}, u32[]{:S(2)}, u32[]{:S(2)}) collective-permute-start(bf16[1024,2816]{1,0:T(8,128)(2,1)} %pad_maximum_fusion), channel_id=1, source_target_pairs={{0,1},{1,0},{2,3},{3,2},{4,5},{5,4},{6,7},{7,6}} | collective-permute-start | bytes 17301512 | tf_op jit(solution)/shard_map/ppermute | solution.py:38
  780.3 341.7 %collective-permute-start.11 = (bf16[2816,1024]{1,0:T(8,128)(2,1)}, bf16[2816,1024]{1,0:T(8,128)(2,1)}, u32[]{:S(2)}, u32[]{:S(2)}) collective-permute-start(bf16[2816,1024]{1,0:T(8,128)(2,1)} %pad_maximum_fusion.1), channel_id=1, source_target_pairs={{0,1},{1,0},{2,3},{3,2},{4,5},{5,4},{6,7},{7,6}} | collective-permute-start | bytes 17301512 | tf_op jit(solution)/shard_map/ppermute | solution.py:39
  843.9 349.6 %collective-permute-start.20 = (bf16[1024,2816]{1,0:T(8,128)(2,1)}, bf16[1024,2816]{1,0:T(8,128)(2,1)}, u32[]{:S(2)}, u32[]{:S(2)}) collective-permute-start(bf16[1024,2816]{1,0:T(8,128)(2,1)} %pad_maximum_fusion.4), channel_id=1, source_target_pairs={{0,1},{1,0},{2,3},{3,2},{4,5},{5,4},{6,7},{7,6}} | collective-permute-start | bytes 17301512 | tf_op jit(solution)/shard_map/ppermute | solution.py:38
  910.5 353.3 %collective-permute-start.23 = (bf16[2816,1024]{1,0:T(8,128)(2,1)}, bf16[2816,1024]{1,0:T(8,128)(2,1)}, u32[]{:S(2)}, u32[]{:S(2)}) collective-permute-start(bf16[2816,1024]{1,0:T(8,128)(2,1)} %pad_maximum_fusion.5), channel_id=1, source_target_pairs={{0,1},{1,0},{2,3},{3,2},{4,5},{5,4},{6,7},{7,6}} | collective-permute-start | bytes 17301512 | tf_op jit(solution)/shard_map/ppermute | solution.py:39
  1343.9 362.6 %collective-permute-start.24 = (bf16[4096,2048]{1,0:T(8,128)(2,1)}, bf16[4096,2048]{1,0:T(8,128)(2,1)S(1)}, u32[]{:S(2)}, u32[]{:S(2)}) collective-permute-start(bf16[4096,2048]{1,0:T(8,128)(2,1)} %add_convert_fusion), channel_id=1, source_target_pairs={{0,4},{4,0},{1,5},{5,1},{2,6},{6,2},{3,7},{7,3}} | collective-permute-start | bytes 50331656 | tf_op jit(solution)/shard_map/ppermute | solution.py:48
  (17 other events, 458.9 us)
